TPU v7x, 32 devices: a whole 2x2x4 slice. The times are simulated.
32 devices in a mesh: lon: 4 (over x, core), lat: 8 (over z, y).
Axes of the slice: x: 2, y: 2, z: 4, core: 2. Of those that a mesh axis runs over, the one named last changes fastest.
Arguments:
- u_vel: float32 [16, 128, 4320], P(None, 'lat', 'lon'), may hold values from -6 to 6
- v_vel: float32 [16, 128, 4320], P(None, 'lat', 'lon'), may hold values from -6 to 6
- u_mask: int32 [16, 128, 4320], P(None, 'lat', 'lon'), may hold values 0 or 1
- v_mask: int32 [16, 128, 4320], P(None, 'lat', 'lon'), may hold values 0 or 1
- t_mask: int32 [16, 128, 4320], P(None, 'lat', 'lon'), may hold values 0 or 1
- bottom: int32 [128, 4320], P('lat', 'lon'), may hold values from 0 to 16
- inv_dx: float32 [128, 4320], P('lat', 'lon'), may hold values from 0.5 to 2
- inv_dy: float32 [128, 4320], P('lat', 'lon'), may hold values from 0.5 to 2
Outputs:
- flux_spectrum: float32 [16, 128, 2160], P(None, ('lat', 'lon'))
All inputs are finite; a program needn't handle non-finite values. No bound on the sum of `u_mask` or of `v_mask` or of `t_mask` on one device may be relied on, other than what follows from the above.
Results may differ from a plain program's by a relative error of at most 0.0003.
Values sent between devices are 32-bit elements; how exact they have to be, the bound alone decides.
A program may use at most 64 MiB of HBM per device.

v0:
```python
import math

import jax
import jax.numpy as jnp
from jax import lax
from jax.sharding import PartitionSpec as P

FA = 60


def from_partner(value, axis, bit):
    mask = 2**bit
    pairs = [(source, source ^ mask) for source in range(lax.axis_size(axis))]
    return lax.ppermute(value, axis, pairs)


def padded_2(block, sides, width, periodic):
    for axis, dim in sides:
        count = lax.axis_size(axis)
        forward = [(i, i + 1) for i in range(count - 1)]
        if periodic:
            forward.append((count - 1, 0))
        backward = [(target, source) for source, target in forward]
        low = lax.ppermute(
            lax.slice_in_dim(block, block.shape[dim] - width, None, axis=dim), axis, forward
        )
        high = lax.ppermute(lax.slice_in_dim(block, 0, width, axis=dim), axis, backward)
        block = jnp.concatenate([low, block, high], axis=dim)
    return block


def angle_table(left_count, right_count, modulus):
    left_index = lax.broadcasted_iota(jnp.int32, (left_count, right_count), 0)
    right_index = lax.broadcasted_iota(jnp.int32, (left_count, right_count), 1)
    index_product = left_index * right_index % modulus
    return 2.0 * math.pi / modulus * index_product.astype(jnp.float32)


def cross_flux(stacked):
    field_count, level_count, row_count, length_total = stacked.shape
    inner_count = level_count * row_count
    batch_cols = field_count * inner_count
    first_factor = FA
    second_factor = length_total // first_factor
    half_second = second_factor // 2
    column_data = jnp.transpose(stacked.reshape(batch_cols, length_total))
    first_angle = angle_table(first_factor, first_factor, first_factor)
    cos_first = jnp.cos(first_angle)
    sin_first = jnp.sin(first_angle)
    shaped = column_data.reshape(first_factor, second_factor, batch_cols)
    section_real = jnp.einsum("ka,anr->nkr", cos_first, shaped, precision=lax.Precision.HIGHEST)
    section_imag = -jnp.einsum("ka,anr->nkr", sin_first, shaped, precision=lax.Precision.HIGHEST)
    twist_angle = angle_table(second_factor, first_factor, length_total)[:, :, None]
    twist_cos = jnp.cos(twist_angle)
    twist_sin = jnp.sin(twist_angle)
    twiddled_real = (section_real * twist_cos + section_imag * twist_sin).reshape(
        second_factor, first_factor, field_count, inner_count
    )
    twiddled_imag = (section_imag * twist_cos - section_real * twist_sin).reshape(
        second_factor, first_factor, field_count, inner_count
    )
    second_angle = angle_table(half_second, second_factor, second_factor)
    cos_second = jnp.cos(second_angle)
    sin_second = jnp.sin(second_angle)

    def transform(field_number):
        part_real = twiddled_real[:, :, field_number, :].reshape(
            second_factor, first_factor * inner_count
        )
        part_imag = twiddled_imag[:, :, field_number, :].reshape(
            second_factor, first_factor * inner_count
        )
        out_real = jnp.dot(cos_second, part_real, precision=lax.Precision.HIGHEST) + jnp.dot(
            sin_second, part_imag, precision=lax.Precision.HIGHEST
        )
        out_imag = jnp.dot(cos_second, part_imag, precision=lax.Precision.HIGHEST) - jnp.dot(
            sin_second, part_real, precision=lax.Precision.HIGHEST
        )
        return (out_real, out_imag)

    real_zero, imag_zero = transform(0)
    real_one, imag_one = transform(1)
    real_two, imag_two = transform(2)
    real_three, imag_three = transform(3)
    cross_terms = (
        real_zero * real_two + imag_zero * imag_two + real_one * real_three + imag_one * imag_three
    )
    wave_count = half_second * first_factor
    cross_terms = cross_terms.reshape(wave_count, inner_count)
    wave_index = lax.broadcasted_iota(jnp.int32, (wave_count, 1), 0)
    weights_m = jnp.where(wave_index == 0, 1.0, 2.0).astype(jnp.float32)
    flux_out = -weights_m * cross_terms / length_total
    return jnp.transpose(flux_out).reshape(level_count, row_count, wave_count)


def body(u_vel, v_vel, u_mask, v_mask, t_mask, bottom, inv_dx, inv_dy):
    level_count, tile_rows, tile_cols = u_vel.shape
    depth_level_index = lax.broadcasted_iota(jnp.int32, (level_count, tile_rows, tile_cols), 0)
    weight = t_mask.astype(jnp.float32) * (depth_level_index < bottom[None]).astype(jnp.float32)
    masked = jnp.stack([u_vel * u_mask.astype(jnp.float32), v_vel * v_mask.astype(jnp.float32)])
    edge_row = -masked[:, :, -1, :]
    lon_count = lax.axis_size("lon")
    partner = edge_row
    for bit_number in range(lon_count.bit_length() - 1):
        partner = from_partner(partner, "lon", bit_number)
    folded = partner[:, :, ::-1]
    padded = padded_2(masked, (("lat", 2),), 1, False)
    at_north = lax.axis_index("lat") == lax.axis_size("lat") - 1
    north_row = jnp.where(at_north, folded, padded[:, :, -1, :])
    padded = jnp.concatenate([padded[:, :, :-1, :], north_row[:, :, None, :]], axis=2)
    slope_lat = (padded[:, :, 2:, :] - padded[:, :, :-2, :]) * 0.5 * inv_dy
    side_halo = padded_2(masked, (("lon", 3),), 1, True)
    slope_lon = (side_halo[..., 2:] - side_halo[..., :-2]) * 0.5 * inv_dx
    advect = weight * (masked[0] * slope_lon + masked[1] * slope_lat)
    packed = jnp.concatenate([masked, advect], axis=0)
    return cross_flux(lax.all_to_all(packed, "lon", split_axis=2, concat_axis=3, tiled=True))


def solution(mesh):
    placed = (
        P(None, "lat", "lon"),
        P(None, "lat", "lon"),
        P(None, "lat", "lon"),
        P(None, "lat", "lon"),
        P(None, "lat", "lon"),
        P("lat", "lon"),
        P("lat", "lon"),
        P("lat", "lon"),
    )
    return jax.shard_map(
        body, mesh=mesh, in_specs=placed, out_specs=P(None, ("lat", "lon"), None), check_vma=False
    )
```

profile of v0, /device:TPU:0, one launch (start us, length us, event | category | flops | bytes accessed | tf_op | source)
XLA Modules:
  0.0 275.1 jit_solution(10475470396212448683)
XLA Ops:
  0.0 3.6 %copy_multiply_fusion = (f32[16,16,1080]{2,0,1:T(8,128)S(1)}, f32[16,16,1080]{2,0,1:T(8,128)S(1)}) fusion(f32[16,16,1080]{2,1,0:T(8,128)} %param.9, s32[16,16,1080]{2,1,0:T(8,128)} %param.11, s32[16,16,1080]{2,1,0:T(8,128)} %param.10, f32[16,16,1080]{2,1,0:T(8,128)} %param.8), kind=kLoop, calls=%fused_computation.39 | loop fusion | flops 1105920 | bytes 6635520 | tf_op jit(solution)/shard_map/mul | solution.py:100
  4.9 5.1 %collective-permute-start.5 = (f32[2,16,1,1080]{3,1,0,2:T(8,128)}, f32[2,16,1,1080]{3,1,0,2:T(8,128)}, u32[]{:S(2)}, u32[]{:S(2)}) collective-permute-start(f32[2,16,1,1080]{3,1,0,2:T(8,128)} %get-tuple-element.6), channel_id=1, source_target_pairs={{0,1},{1,2},{2,3},{3,4},{4,5},{5,6},{6,7},{8,9},{9,10},{10,11},{11... | collective-permute-start | bytes 414728 | tf_op jit(solution)/shard_map/ppermute | solution.py:24
  17.8 6.1 %collective-permute-done.3 = f32[2,16,1080]{2,1,0:T(8,128)} collective-permute-done((f32[2,16,1080]{2,1,0:T(8,128)}, f32[2,16,1080]{2,1,0:T(8,128)}, u32[]{:S(2)}, u32[]{:S(2)}) %collective-permute-start.3) | collective-permute-done | bytes 138272 | tf_op jit(solution)/shard_map/ppermute | solution.py:14
  23.8 5.0 %reverse = f32[2,16,1152]{2,1,0:T(8,128)} reverse(f32[2,16,1152]{2,1,0:T(8,128)} %bitcast.47), dimensions={2} | reverse | bytes 294912
  29.9 3.5 %fusion.15 = f32[2,16,16,1080]{3,1,0,2:T(8,128)S(1)} fusion(f32[2,16,1,1080]{3,1,0,2:T(8,128)} %collective-permute-done.5, f32[1,16,16,1080]{3,1,0,2:T(8,128)S(1)} %bitcast.73, f32[1,16,16,1080]{3,1,0,2:T(8,128)S(1)} %bitcast.77, f32[2,16,1,1080]{3,1,0,2:T(8,128)S(1)} %fusion.19, f32[2,16,16,1]{3,1,0,2:T(8,128)} %collective-permute-done.1, ...), kind=kLoop, calls=%fused_computation.28 | loop fusion | flops 8847360 | bytes 8160256 | tf_op jit(solution)/shard_map/mul | solution.py:114
  33.4 2.6 pad_maximum_fusion
  36.0 5.5 %all-to-all-start = ((f32[4,16,16,1080]{3,1,0,2:T(8,128)}), f32[4,16,16,1080]{3,1,0,2:T(8,128)}, u32[]{:S(2)}, u32[]{:S(2)}) async-start(f32[4,16,16,1080]{3,1,0,2:T(8,128)} %pad_maximum_fusion), calls=%async_computation | async-start | bytes 9437184 | tf_op jit(solution)/shard_map/all_to_all | solution.py:116
  41.7 53.9 %all-to-all-done = f32[4,16,16,1080]{3,1,0,2:T(8,128)} async-done(((f32[4,16,16,1080]{3,1,0,2:T(8,128)}), f32[4,16,16,1080]{3,1,0,2:T(8,128)}, u32[]{:S(2)}, u32[]{:S(2)}) %all-to-all-start) | async-done | bytes 4423712 | tf_op jit(solution)/shard_map/all_to_all | solution.py:116
  95.6 7.5 %copy.84 = f32[4,16,4,4,1080]{4,2,3,1,0:T(4,128)} copy(f32[4,16,4,4,1080]{4,1,0,3,2:T(8,128)} %bitcast.5) | data formatting | bytes 8847360 | tf_op jit(solution)/shard_map/all_to_all | solution.py:116
  103.2 6.1 %reshape.58 = f32[256,4320]{1,0:T(8,128)} reshape(f32[4,16,4,4,1080]{4,3,2,1,0:T(4,128)} %bitcast.79) | data formatting | bytes 8847360 | tf_op jit(solution)/shard_map/reshape | solution.py:46
  109.3 5.8 %copy.55 = f32[4320,256]{1,0:T(8,128)} copy(f32[4320,256]{0,1:T(8,128)} %bitcast.80) | data formatting | bytes 8847360 | tf_op jit(solution)/shard_map/transpose | solution.py:46
  115.0 7.8 %fusion.7 = f32[72,256,60]{1,2,0:T(8,128)S(1)} fusion(f32[60,72,256]{2,1,0:T(8,128)} %bitcast.67), kind=kOutput, calls=%fused_computation.19 | convolution fusion | flops 796294784 | bytes 8847360 | tf_op jit(solution)/shard_map/ka,anr->nkr/dot_general | solution.py:52
  122.9 10.1 %add_bitcast_fusion = (f32[72,60,256]{2,1,0:T(8,128)S(1)}, f32[72,60,256]{2,1,0:T(8,128)}) fusion(f32[72,256,60]{1,2,0:T(8,128)S(1)} %fusion.7, f32[72,60]{1,0:T(8,128)S(1)} %get-tuple-element.24, f32[72,60]{1,0:T(8,128)S(1)} %get-tuple-element.25, f32[60,72,256]{2,1,0:T(8,128)S(1)} %bitcast.70), kind=kOutput, calls=%fused_computation.3 | convolution fusion | flops 804036224 | bytes 17729280 | tf_op jit(solution)/shard_map/ka,anr->nkr/dot_general | solution.py:51
  133.0 4.6 %copy.58 = f32[72,60,256]{2,0,1:T(8,128)} copy(f32[72,60,256]{2,1,0:T(8,128)S(1)} %get-tuple-element.7) | data formatting | bytes 8847360 | tf_op jit(solution)/shard_map/add | solution.py:56
  137.6 8.4 %reshape.60 = f32[72,60,4,64]{3,2,0,1:T(4,128)} reshape(f32[72,60,256]{2,0,1:T(8,128)} %copy.58) | data formatting | bytes 8847360 | tf_op jit(solution)/shard_map/reshape | solution.py:56
  146.0 21.7 %fusion.177 = (f32[72,60,1,64]{3,2,0,1:T(1,128)S(1)}, f32[72,60,1,64]{3,2,0,1:T(1,128)}, f32[72,60,1,64]{3,2,0,1:T(1,128)}, f32[72,60,1,64]{3,2,0,1:T(1,128)}) fusion(f32[72,60,4,64]{3,2,0,1:T(4,128)} %reshape.60), kind=kLoop, calls=%fused_computation.184 | loop fusion | bytes 8847360 | tf_op jit(solution)/shard_map/slice | solution.py:67
  170.4 3.5 %copy.66 = f32[72,60,1,64]{3,1,0,2:T(8,128)} copy(f32[72,60,1,64]{3,2,0,1:T(1,128)} %get-tuple-element.10) | data formatting | bytes 2211840 | tf_op jit(solution)/shard_map/slice | solution.py:67
  173.9 2.2 reshape_squeeze.30
  177.7 3.5 %copy.64 = f32[72,60,1,64]{3,1,0,2:T(8,128)} copy(f32[72,60,1,64]{3,2,0,1:T(1,128)} %get-tuple-element.11) | data formatting | bytes 2211840 | tf_op jit(solution)/shard_map/slice | solution.py:67
  185.0 3.5 %copy.62 = f32[72,60,1,64]{3,1,0,2:T(8,128)} copy(f32[72,60,1,64]{3,2,0,1:T(1,128)} %get-tuple-element.12) | data formatting | bytes 2211840 | tf_op jit(solution)/shard_map/slice | solution.py:67
  188.5 2.4 reshape_squeeze.26
  192.5 6.9 %copy.60 = f32[72,60,256]{2,0,1:T(8,128)} copy(f32[72,60,256]{2,1,0:T(8,128)} %get-tuple-element.8) | data formatting | bytes 8847360 | tf_op jit(solution)/shard_map/sub | solution.py:59
  199.4 8.4 %reshape.61 = f32[72,60,4,64]{3,2,0,1:T(4,128)} reshape(f32[72,60,256]{2,0,1:T(8,128)} %copy.60) | data formatting | bytes 8847360 | tf_op jit(solution)/shard_map/reshape | solution.py:59
  207.8 21.6 %fusion.178 = (f32[72,60,1,64]{3,2,0,1:T(1,128)S(1)}, f32[72,60,1,64]{3,2,0,1:T(1,128)}, f32[72,60,1,64]{3,2,0,1:T(1,128)}, f32[72,60,1,64]{3,2,0,1:T(1,128)}) fusion(f32[72,60,4,64]{3,2,0,1:T(4,128)} %reshape.61), kind=kLoop, calls=%fused_computation.185 | loop fusion | bytes 8847360 | tf_op jit(solution)/shard_map/slice | solution.py:70
  231.3 2.9 %reshape_squeeze.25 = f32[72,3840]{1,0:T(8,128)} reshape(f32[72,60,1,64]{3,1,0,2:T(8,128)} %copy.61) | data formatting | bytes 2211840 | tf_op jit(solution)/shard_map/reshape;squeeze | solution.py:70
  234.2 2.8 %fusion.54 = f32[36,3840]{1,0:T(8,128)} fusion(f32[72,3840]{1,0:T(8,128)} %reshape_squeeze.25), kind=kOutput, calls=%fused_computation.88 | convolution fusion | flops 119462688 | bytes 1658880 | tf_op jit(solution)/shard_map/dot_general | solution.py:76
  237.1 3.5 %copy.67 = f32[72,60,1,64]{3,1,0,2:T(8,128)} copy(f32[72,60,1,64]{3,2,0,1:T(1,128)} %get-tuple-element.14) | data formatting | bytes 2211840 | tf_op jit(solution)/shard_map/slice | solution.py:70
  240.6 3.2 %reshape_squeeze.31 = f32[72,3840]{1,0:T(8,128)} reshape(f32[72,60,1,64]{3,1,0,2:T(8,128)} %copy.67) | data formatting | bytes 2211840 | tf_op jit(solution)/shard_map/reshape;squeeze | solution.py:70
  251.0 2.9 %reshape_squeeze.29 = f32[72,3840]{1,0:T(8,128)} reshape(f32[72,60,1,64]{3,1,0,2:T(8,128)} %copy.65) | data formatting | bytes 2211840 | tf_op jit(solution)/shard_map/reshape;squeeze | solution.py:70
  254.0 2.8 %fusion.46 = f32[36,3840]{1,0:T(8,128)} fusion(f32[72,3840]{1,0:T(8,128)} %reshape_squeeze.29), kind=kOutput, calls=%fused_computation.84 | convolution fusion | flops 119462688 | bytes 1658880 | tf_op jit(solution)/shard_map/dot_general | solution.py:76
  256.8 3.5 %copy.63 = f32[72,60,1,64]{3,1,0,2:T(8,128)} copy(f32[72,60,1,64]{3,2,0,1:T(1,128)} %get-tuple-element.16) | data formatting | bytes 2211840 | tf_op jit(solution)/shard_map/slice | solution.py:70
  260.3 3.2 %reshape_squeeze.27 = f32[72,3840]{1,0:T(8,128)} reshape(f32[72,60,1,64]{3,1,0,2:T(8,128)} %copy.63) | data formatting | bytes 2211840 | tf_op jit(solution)/shard_map/reshape;squeeze | solution.py:70
  (84 shorter events, 40.0 us)
Async XLA Ops:
  4.4 10.4 %collective-permute-start.2 = (f32[2,16,1080]{2,1,0:T(8,128)S(1)}, f32[2,16,1080]{2,1,0:T(8,128)}, u32[]{:S(2)}, u32[]{:S(2)}) collective-permute-start(f32[2,16,1080]{2,1,0:T(8,128)S(1)} %get-tuple-element.5), channel_id=1, source_target_pairs={{0,8},{8,0},{16,24},{24,16},{1,9},{9,1},{17,25},{25,17},{2,10},{10... | collective-permute-start | bytes 414728 | tf_op jit(solution)/shard_map/ppermute | solution.py:14
  4.9 25.0 %collective-permute-start.5 = (f32[2,16,1,1080]{3,1,0,2:T(8,128)}, f32[2,16,1,1080]{3,1,0,2:T(8,128)}, u32[]{:S(2)}, u32[]{:S(2)}) collective-permute-start(f32[2,16,1,1080]{3,1,0,2:T(8,128)} %get-tuple-element.6), channel_id=1, source_target_pairs={{0,1},{1,2},{2,3},{3,4},{4,5},{5,6},{6,7},{8,9},{9,10},{10,11},{11... | collective-permute-start | bytes 414728 | tf_op jit(solution)/shard_map/ppermute | solution.py:24
  10.0 3.6 %copy-start.15 = (s32[16,16,1080]{2,1,0:T(8,128)S(1)}, s32[16,16,1080]{2,1,0:T(8,128)}, u32[]{:S(2)}) copy-start(s32[16,16,1080]{2,1,0:T(8,128)} %param.12) | copy-start | bytes 3317764
  10.0 3.6 %copy-start.16 = (s32[16,1080]{1,0:T(8,128)S(1)}, s32[16,1080]{1,0:T(8,128)}, u32[]{:S(2)}) copy-start(s32[16,1080]{1,0:T(8,128)} %param.13) | copy-start | bytes 207364
  10.0 18.8 %collective-permute-start.4 = (f32[2,16,1,1080]{3,1,0,2:T(8,128)}, f32[2,16,1,1080]{3,1,0,2:T(8,128)}, u32[]{:S(2)}, u32[]{:S(2)}) collective-permute-start(f32[2,16,1,1080]{3,1,0,2:T(8,128)} %get-tuple-element.19), channel_id=1, source_target_pairs={{1,0},{2,1},{3,2},{4,3},{5,4},{6,5},{7,6},{9,8},{10,9},{11,10},{12... | collective-permute-start | bytes 414728 | tf_op jit(solution)/shard_map/ppermute | solution.py:27
  12.2 17.7 %collective-permute-start = (f32[2,16,16,1]{3,1,0,2:T(8,128)}, f32[2,16,16,1]{3,1,0,2:T(8,128)}, u32[]{:S(2)}, u32[]{:S(2)}) collective-permute-start(f32[2,16,16,1]{3,1,0,2:T(8,128)} %get-tuple-element.17), channel_id=1, source_target_pairs={{8,0},{16,8},{24,16},{0,24},{9,1},{17,9},{25,17},{1,25},{10,2},{18... | collective-permute-start | bytes 6152 | tf_op jit(solution)/shard_map/ppermute | solution.py:27
  13.6 1.9 copy-start.17
  13.6 1.9 copy-start.18
  13.6 16.3 %collective-permute-start.1 = (f32[2,16,16,1]{3,1,0,2:T(8,128)}, f32[2,16,16,1]{3,1,0,2:T(8,128)}, u32[]{:S(2)}, u32[]{:S(2)}) collective-permute-start(f32[2,16,16,1]{3,1,0,2:T(8,128)} %get-tuple-element.18), channel_id=1, source_target_pairs={{0,8},{8,16},{16,24},{24,0},{1,9},{9,17},{17,25},{25,1},{2,10},{10... | collective-permute-start | bytes 6152 | tf_op jit(solution)/shard_map/ppermute | solution.py:24
  14.8 9.0 %collective-permute-start.3 = (f32[2,16,1080]{2,1,0:T(8,128)}, f32[2,16,1080]{2,1,0:T(8,128)}, u32[]{:S(2)}, u32[]{:S(2)}) collective-permute-start(f32[2,16,1080]{2,1,0:T(8,128)} %collective-permute-done.2), channel_id=1, source_target_pairs={{0,16},{8,24},{16,0},{24,8},{1,17},{9,25},{17,1},{25,9},{2,18},{10... | collective-permute-start | bytes 414728 | tf_op jit(solution)/shard_map/ppermute | solution.py:14
  36.0 59.6 %all-to-all-start = ((f32[4,16,16,1080]{3,1,0,2:T(8,128)}), f32[4,16,16,1080]{3,1,0,2:T(8,128)}, u32[]{:S(2)}, u32[]{:S(2)}) async-start(f32[4,16,16,1080]{3,1,0,2:T(8,128)} %pad_maximum_fusion), calls=%async_computation | async-start | bytes 9437184 | tf_op jit(solution)/shard_map/all_to_all | solution.py:116
  115.0 7.8 %slice-start = ((s8[4423680]{0:T(1024)(128)(4,1)}), s8[4194304]{0:T(1024)(128)(4,1)S(1)}, s32[]{:S(2)}) async-start(s8[4423680]{0:T(1024)(128)(4,1)} %bitcast.68), calls=%async_computation.1 | async-start | bytes 8388608
  115.0 7.8 %slice-start.1 = ((s8[4423680]{0:T(1024)(128)(4,1)}), s8[229376]{0:T(1024)(128)(4,1)S(1)}, s32[]{:S(2)}) async-start(s8[4423680]{0:T(1024)(128)(4,1)} %bitcast.68), calls=%async_computation.2 | async-start | bytes 458752
  176.1 1.6 copy-start.1
  243.8 2.2 copy-start.4
  243.8 2.2 copy-start.11
  245.9 1.6 copy-start.2
  247.6 1.6 copy-start.6
  263.5 2.2 copy-start.5
  263.5 2.2 copy-start.9
  266.5 1.2 copy-start.3
  266.5 1.4 copy-start.8
  266.5 1.6 copy-start.13
  268.1 1.1 copy-start.12
  268.1 1.3 copy-start.14
  269.3 1.1 copy-start.10
  270.4 1.2 copy-start
  270.4 1.4 copy-start.7
where the time goes:
time: 280 us; the launch traced here: 275 us
  local copies, waits for them, and re-layouts  143 us (51%)
  waiting for transfers between devices  60 us (21%)
  matrix products  42.2 us (15%)
  other arithmetic  14.8 us (5%)
  starting transfers between devices  14.5 us (5%)
    all_to_all x1, waiting for transfers between devices, body(): lax.all_to_all(packed, 'lon', split_axis=2, concat_axis=3, tiled=True)  53.9 us
    slice x5, local copies, waits for them, and re-layouts, transform(): twiddled_real[:, :, field_number, :]  32.6 us
    slice x5, local copies, waits for them, and re-layouts, transform(): twiddled_imag[:, :, field_number, :]  32.3 us
    another operation x4, local copies, waits for them, and re-layouts, transform(): twiddled_imag[:, :, field_number, :]  12.3 us
    dot_general x1, matrix products, cross_flux(): jnp.einsum('ka,anr->nkr', cos_first, shaped, precision=lax.Precision.HIGH...  10.1 us
    dot_general x4, matrix products, transform(): jnp.dot(cos_second, part_imag, precision=lax.Precision.HIGHEST)  9.92 us
    reshape x1, local copies, waits for them, and re-layouts, cross_flux(): (section_real * twist_cos + section_imag * twist_sin).reshape(second_fact...  8.37 us
    reshape x1, local copies, waits for them, and re-layouts, cross_flux(): (section_imag * twist_cos - section_real * twist_sin).reshape(second_fact...  8.37 us
  transfers between devices with their start and end apart: 7, of which 2 were waited for; matrix products, arithmetic and copies ran while one was open for 4% of the time, Pallas kernels for 0%

commit v1 on v0

v1 whole, which is shorter than its diff:
```python
import functools

import jax
import jax.numpy as jnp
import numpy as np
from jax import lax
from jax.experimental import pallas as pl
from jax.experimental.pallas import tpu as pltpu
from jax.sharding import PartitionSpec as P

MESH = pl.DeviceIdType.MESH


def up(value, step):
    return -(-value // step) * step


def split_pair(table):
    high = table.astype(jnp.bfloat16)
    low = (table - high.astype(np.float64)).astype(jnp.bfloat16)
    return high, low


class Plan:
    def __init__(self, lon_count, lat_count, levels, rows, cols):
        self.L, self.T, self.K, self.J, self.W = lon_count, lat_count, levels, rows, cols
        self.NI = cols * lon_count
        self.R = rows // lon_count
        best = None
        for n2 in range(2, cols + 1, 2):
            n1 = self.NI // n2
            if cols % n2 or n1 % 4:
                continue
            cost = abs(n1 - 60)
            if best is None or cost < best[0]:
                best = (cost, n2)
        self.N2 = best[1]
        self.N1 = self.NI // self.N2
        self.A = cols // self.N2
        self.AP = up(self.A, 8)
        self.KA = lon_count * self.AP
        self.KO = up(self.N1, 8)
        self.NP = up(self.N2, 8)
        self.PH = self.N2 // 2
        self.U = 4 if self.N2 % 4 == 0 else 2
        self.PO = up(self.PH, 8)
        self.NM = self.NI // 2
        self.WL = up(cols, 128)
        self.WP = up(cols, 8)
        self.B = self.R * levels
        self.LN = up(2 * self.B, 128)
        self.PR = self.AP * self.N2

    def tables(self):
        n = np.arange(self.N2)[:, None, None]
        k = np.arange(self.N1)[None, :, None]
        a = np.arange(self.N1)[None, None, :]
        angle = 2 * np.pi / self.NI * ((k * (self.N2 * a + n)) % self.NI)
        real = np.zeros((self.N2, self.KO, self.L, self.AP))
        imag = np.zeros_like(real)
        real[:, : self.N1, :, : self.A] = np.cos(angle).reshape(self.N2, self.N1, self.L, self.A)
        imag[:, : self.N1, :, : self.A] = -np.sin(angle).reshape(self.N2, self.N1, self.L, self.A)
        first = np.concatenate([real, imag], axis=1).reshape(self.N2, 2 * self.KO, self.KA)
        high, low = split_pair(first)
        first = np.concatenate([high, low], axis=2)
        p = np.arange(self.PH)[:, None]
        m = np.arange(self.N2)[None, :]
        angle = 2 * np.pi / self.N2 * ((p * m) % self.N2)
        second = np.zeros((2, self.PO, 2, self.NP))
        second[0, : self.PH, 0, : self.N2] = np.cos(angle)
        second[0, : self.PH, 1, : self.N2] = np.sin(angle)
        second[1, : self.PH, 0, : self.N2] = -np.sin(angle)
        second[1, : self.PH, 1, : self.N2] = np.cos(angle)
        second = second.reshape(2 * self.PO, 2 * self.NP)
        high, low = split_pair(second)
        second = np.concatenate([high, low, high], axis=1)
        return first, second


def halves(value):
    high = value.astype(jnp.bfloat16)
    low = (value - high.astype(jnp.float32)).astype(jnp.bfloat16)
    return high, low


def kernel(
    p, u_ref, v_ref, um_ref, vm_ref, tm_ref, bot_ref, idx_ref, idy_ref, t1_hbm, t2_ref, out_ref,
    mj, adv, inv, south, north, fold, col_out, col_in, send_a, send_b, got_a, got_b, y_ref,
    f_ref, g_ref, t1, table_sem, halo_send, halo_recv, col_send, col_recv, a_send, a_recv,
    b_send, b_recv,
):
    L, K, J, W, WL = p.L, p.K, p.J, p.W, p.WL
    me = lax.axis_index("lon")
    row = lax.axis_index("lat")
    up_lat, down_lat = lax.rem(row + 1, p.T), lax.rem(row + p.T - 1, p.T)
    right, left = lax.rem(me + 1, L), lax.rem(me + L - 1, L)
    partner = L - 1 - me
    at_north = row == p.T - 1

    table_copy = pltpu.make_async_copy(t1_hbm, t1, table_sem)
    table_copy.start()

    barrier = pltpu.get_barrier_semaphore()
    for off in range(1, L):
        pl.semaphore_signal(
            barrier, inc=1, device_id={"lon": lax.rem(me + off, L)}, device_id_type=MESH
        )
    for other in (up_lat, down_lat):
        pl.semaphore_signal(barrier, inc=1, device_id={"lat": other}, device_id_type=MESH)

    if WL > W:
        tail = jnp.zeros((2, J, K, WL - W), jnp.float32)
        mj[:, :, :, W:] = tail
        adv[:, :, :, W:] = tail
        inv[:, :, W:] = jnp.zeros((2, J, WL - W), jnp.float32)
    inv[0, :, :W] = idx_ref[...] * 0.5
    inv[1, :, :W] = idy_ref[...] * 0.5
    col_out[...] = jnp.zeros_like(col_out)
    for j in range(J):
        mj[0, j, :, :W] = u_ref[:, j, :] * um_ref[:, j, :].astype(jnp.float32)
        mj[1, j, :, :W] = v_ref[:, j, :] * vm_ref[:, j, :].astype(jnp.float32)
    for j in range(J):
        for f in range(2):
            col_out[0, f * K : (f + 1) * K, j : j + 1] = mj[f, j, :, W - 1 : W]
            col_out[1, f * K : (f + 1) * K, j : j + 1] = mj[f, j, :, 0:1]
    pl.semaphore_wait(barrier, L + 1)

    def remote(src, dst, send, recv, device):
        return pltpu.make_async_remote_copy(
            src_ref=src, dst_ref=dst, send_sem=send, recv_sem=recv, device_id=device,
            device_id_type=MESH,
        )

    to_north = remote(mj.at[:, J - 1], south, halo_send.at[0], halo_recv.at[0], {"lat": up_lat})
    to_south = remote(mj.at[:, 0], north, halo_send.at[1], halo_recv.at[1], {"lat": down_lat})
    to_fold = remote(mj.at[:, J - 1], fold, halo_send.at[2], halo_recv.at[2], {"lon": partner})
    to_right = remote(col_out.at[0], col_in.at[0], col_send.at[0], col_recv.at[0], {"lon": right})
    to_left = remote(col_out.at[1], col_in.at[1], col_send.at[1], col_recv.at[1], {"lon": left})
    to_north.start()
    to_south.start()
    to_right.start()
    to_left.start()

    @pl.when(at_north)
    def _():
        to_fold.start()

    def turn(source, target, dest):
        for start in range(0, W, 128):
            pieces = [
                source[f, dest * p.R + r, :, start : start + 128]
                for f in range(2)
                for r in range(p.R)
            ]
            if p.LN > 2 * p.B:
                pieces.append(jnp.zeros((p.LN - 2 * p.B, 128), jnp.float32))
            turned = jnp.transpose(jnp.concatenate(pieces, axis=0))
            size = min(128, p.WP - start)
            target[start : start + size, :] = turned[:size]

    order = sorted(range(1, L), key=lambda off: abs(off - L // 2))

    def exchange(source, buffer, got, send, recv):
        copies = []
        for slot, off in enumerate(order):
            dest = lax.rem(me + off, L)
            turn(source, buffer.at[slot], dest)
            copy = remote(
                buffer.at[slot], got.at[me, pl.ds(0, p.WP)], send.at[slot], recv.at[slot],
                {"lon": dest},
            )
            copy.start()
            copies.append(copy)
        turn(source, got.at[me], me)
        return copies

    if p.PR > p.WP:
        pad = jnp.zeros((L, p.PR - p.WP, p.LN), jnp.float32)
        got_a[:, p.WP :, :] = pad
        got_b[:, p.WP :, :] = pad
    copies_a = exchange(mj, send_a, got_a, a_send, a_recv)

    to_north.wait()
    to_south.wait()
    to_right.wait()
    to_left.wait()

    @pl.when(at_north)
    def _():
        to_fold.wait()
        line = lax.broadcasted_iota(jnp.int32, (128, 128), 0)
        lane = lax.broadcasted_iota(jnp.int32, (128, 128), 1)
        flip = (line + lane == 127).astype(jnp.float32)
        value = fold[...].reshape(2 * K, WL)
        blocks = [
            jnp.dot(
                value[:, start : start + 128], flip, precision=lax.Precision.HIGHEST,
                preferred_element_type=jnp.float32,
            )
            for start in range(WL - 128, -1, -128)
        ]
        turned = jnp.concatenate(blocks, axis=1)
        if WL > W:
            turned = pltpu.roll(turned, W, 1)
        north[...] = -turned.reshape(2, K, WL)

    @pl.when(row == 0)
    def _():
        south[...] = jnp.zeros_like(south)

    lane = lax.broadcasted_iota(jnp.int32, (K, WL), 1)
    level = lax.broadcasted_iota(jnp.int32, (K, W), 0)
    for j in range(J):
        here = [mj[f, j] for f in range(2)]
        inv_x = inv[0, j : j + 1, :]
        inv_y = inv[1, j : j + 1, :]
        live = level < bot_ref[j : j + 1, :]
        weight = jnp.where(live, tm_ref[:, j, :].astype(jnp.float32), 0.0)
        for f in range(2):
            below = south[f] if j == 0 else mj[f, j - 1]
            above = north[f] if j == J - 1 else mj[f, j + 1]
            west = jnp.where(
                lane == 0, col_in[0, f * K : (f + 1) * K, j : j + 1], pltpu.roll(here[f], 1, 1)
            )
            east = jnp.where(
                lane == W - 1, col_in[1, f * K : (f + 1) * K, j : j + 1],
                pltpu.roll(here[f], WL - 1, 1),
            )
            slope_x = (east - west) * inv_x
            slope_y = (above - below) * inv_y
            total = here[0] * slope_x + here[1] * slope_y
            adv[f, j, :, :W] = weight * total[:, :W]

    copies_b = exchange(adv, send_b, got_b, b_send, b_recv)

    if p.NP > p.N2:
        y_ref[p.N2 * 2 * p.KO :, :] = jnp.zeros(
            ((p.NP - p.N2) * 2 * p.KO, p.LN), jnp.float32
        )
    table_copy.wait()

    def first_stage(got):
        def step(block, carry):
            for part in range(p.U):
                n = block * p.U + part
                x = jnp.concatenate(
                    [got[s, pl.ds(n, p.AP, stride=p.N2), :] for s in range(L)], axis=0
                )
                high, low = halves(x)
                data = jnp.concatenate([high, high, low, low], axis=0)
                table = t1[n]
                out = jnp.dot(
                    jnp.concatenate([table, table], axis=1), data,
                    preferred_element_type=jnp.float32,
                )
                y_ref[pl.ds(pl.multiple_of(n * 2 * p.KO, 8), 2 * p.KO), :] = out
            return carry

        lax.fori_loop(0, p.N2 // p.U, step, 0)

    def second_stage(finish):
        table = t2_ref[...]

        def step(block, carry):
            for part in range(2):
                ks = [block * 4 + part * 2 + q for q in range(2)]
                sides = []
                for k in ks:
                    y = jnp.concatenate(
                        [
                            y_ref[pl.ds(k + c * p.KO, p.NP, stride=2 * p.KO), :]
                            for c in range(2)
                        ],
                        axis=0,
                    )
                    high, low = halves(y)
                    sides.append(jnp.concatenate([high, high, low], axis=0))
                out = jnp.dot(
                    table, jnp.concatenate(sides, axis=1), preferred_element_type=jnp.float32
                )
                for q, k in enumerate(ks):
                    finish(k, out[:, q * p.LN : (q + 1) * p.LN])
            return carry

        lax.fori_loop(0, p.N1 // 4, step, 0)

    def keep(k, value):
        f_ref[k] = value

    def cross(k, value):
        both = f_ref[k] * value
        g_ref[pl.ds(k, p.PO, stride=p.N1), :] = both[: p.PO] + both[p.PO :]

    for copy in copies_a:
        copy.wait()
    first_stage(got_a)
    second_stage(keep)
    for copy in copies_b:
        copy.wait()
    first_stage(got_b)
    second_stage(cross)

    for start in range(0, p.NM, 128):
        size = min(128, p.NM - start)
        block = jnp.transpose(g_ref[start : start + 128, :])
        wave = lax.broadcasted_iota(jnp.int32, (p.B, 128), 1) + start
        scale = jnp.where(wave == 0, -1.0 / p.NI, -2.0 / p.NI)
        total = (block[: p.B] + block[p.B : 2 * p.B]) * scale
        out_ref[:, start : start + size] = total[:, :size]


def body(p, *args):
    first, second = p.tables()
    f32 = jnp.float32
    vmem = pl.BlockSpec(memory_space=pltpu.VMEM)
    dma = pltpu.SemaphoreType.DMA
    out = pl.pallas_call(
        functools.partial(kernel, p),
        out_shape=jax.ShapeDtypeStruct((p.B, p.NM), f32),
        in_specs=[vmem] * 8 + [pl.BlockSpec(memory_space=pl.ANY), vmem],
        out_specs=vmem,
        scratch_shapes=[
            pltpu.VMEM((2, p.J, p.K, p.WL), f32),
            pltpu.VMEM((2, p.J, p.K, p.WL), f32),
            pltpu.VMEM((2, p.J, p.WL), f32),
            pltpu.VMEM((2, p.K, p.WL), f32),
            pltpu.VMEM((2, p.K, p.WL), f32),
            pltpu.VMEM((2, p.K, p.WL), f32),
            pltpu.VMEM((2, 2 * p.K, 128), f32),
            pltpu.VMEM((2, 2 * p.K, 128), f32),
            pltpu.VMEM((p.L - 1, p.WP, p.LN), f32),
            pltpu.VMEM((p.L - 1, p.WP, p.LN), f32),
            pltpu.VMEM((p.L, p.PR, p.LN), f32),
            pltpu.VMEM((p.L, p.PR, p.LN), f32),
            pltpu.VMEM((p.NP * 2 * p.KO, p.LN), f32),
            pltpu.VMEM((p.N1, 2 * p.PO, p.LN), f32),
            pltpu.VMEM((max(p.PO * p.N1, up(p.NM, 128)), p.LN), f32),
            pltpu.VMEM((p.N2, 2 * p.KO, 2 * p.KA), jnp.bfloat16),
            dma(()),
            dma((3,)),
            dma((3,)),
            dma((2,)),
            dma((2,)),
            dma((p.L - 1,)),
            dma((p.L - 1,)),
            dma((p.L - 1,)),
            dma((p.L - 1,)),
        ],
        compiler_params=pltpu.CompilerParams(
            collective_id=0, has_side_effects=True, vmem_limit_bytes=62 * 1024 * 1024
        ),
    )(*args, jnp.asarray(first), jnp.asarray(second))
    return jnp.transpose(out.reshape(p.R, p.K, p.NM), (1, 0, 2))


def solution(mesh):
    field = P(None, "lat", "lon")
    flat = P("lat", "lon")

    def run(*args):
        levels, rows, cols = args[0].shape
        plan = Plan(mesh.shape["lon"], mesh.shape["lat"], levels, rows, cols)
        return body(plan, *args)

    return jax.shard_map(
        run, mesh=mesh, in_specs=(field,) * 5 + (flat,) * 3,
        out_specs=P(None, ("lat", "lon"), None), check_vma=False,
    )
```

time: 280 us -> 70.9 us (0.25)
  the two profiles are of different devices: /device:TPU:0 before, /device:TPU:1 now
where the time goes in v1:
time: 70.9 us; the launch traced here: 70.8 us
  Pallas kernels  68.7 us (97%)
  local copies, waits for them, and re-layouts  2.07 us (3%)
    pallas_call x1, Pallas kernels, body(): pl.pallas_call(functools.partial(kernel, p), out_shape=jax.ShapeDtypeStru...  68.7 us
    reshape x1, local copies, waits for them, and re-layouts, body(): return jnp.transpose(out.reshape(p.R, p.K, p.NM), (1, 0, 2))  2.07 us

profile of v1, /device:TPU:1, one launch (start us, length us, event | category | flops | bytes accessed | tf_op | source)
XLA Modules:
  0.0 70.8 jit_solution(693817756275686714)
XLA Ops:
  0.0 68.7 %shard_map.100 = f32[64,2160]{1,0:T(8,128)} custom-call(f32[16,16,1080]{2,1,0:T(8,128)} %u_ref.1, f32[16,16,1080]{2,1,0:T(8,128)} %v_ref.1, s32[16,16,1080]{2,1,0:T(8,128)} %um_ref.1, s32[16,16,1080]{2,1,0:T(8,128)} %vm_ref.1, s32[16,16,1080]{2,1,0:T(8,128)} %tm_ref.1, s32[16,1080]{1,0:T(8,128)} %bot_ref.1, f32[16,1080]{1,0:T(8,128)} %idx_ref.1, ...), custom_call_target="tpu_custom_call" | custom-call | tf_op jit(solution)/shard_map/pallas_call | solution.py:317
  68.7 2.1 %copy.13 = f32[4,16,2160]{2,0,1:T(4,128)} copy(f32[4,16,2160]{2,1,0:T(8,128)} %bitcast.4) | data formatting | bytes 1105920 | tf_op jit(solution)/shard_map/reshape | solution.py:353

commit v2 on v1

--- a/solution.py
+++ b/solution.py
@@ -42,6 +42,7 @@
         self.KO = up(self.N1, 8)
         self.NP = up(self.N2, 8)
         self.PH = self.N2 // 2
+        self.C = 3 if self.N2 % 24 == 0 and cols % 8 == 0 else 1
         self.U = 4 if self.N2 % 4 == 0 else 2
         self.PO = up(self.PH, 8)
         self.NM = self.NI // 2
@@ -86,7 +87,7 @@
 def kernel(
     p, u_ref, v_ref, um_ref, vm_ref, tm_ref, bot_ref, idx_ref, idy_ref, t1_hbm, t2_ref, out_ref,
     mj, adv, inv, south, north, fold, col_out, col_in, send_a, send_b, got_a, got_b, y_ref,
-    f_ref, g_ref, t1, table_sem, halo_send, halo_recv, col_send, col_recv, a_send, a_recv,
+    f_ref, g_ref, turned_out, t1, table_sem, halo_send, halo_recv, col_send, col_recv, a_send, a_recv,
     b_send, b_recv,
 ):
     L, K, J, W, WL = p.L, p.K, p.J, p.W, p.WL
@@ -160,17 +161,27 @@
 
     order = sorted(range(1, L), key=lambda off: abs(off - L // 2))
 
-    def exchange(source, buffer, got, send, recv):
-        copies = []
+    def exchange(source, buffer, got, send, recv, chunks):
+        copies = [[] for _ in range(chunks)]
+        width = p.N2 // chunks
         for slot, off in enumerate(order):
             dest = lax.rem(me + off, L)
             turn(source, buffer.at[slot], dest)
-            copy = remote(
-                buffer.at[slot], got.at[me, pl.ds(0, p.WP)], send.at[slot], recv.at[slot],
-                {"lon": dest},
-            )
-            copy.start()
-            copies.append(copy)
+            for c in range(chunks):
+                if chunks == 1:
+                    src, dst = buffer.at[slot], got.at[me, pl.ds(0, p.WP)]
+                else:
+                    part = pl.ds(c * width, width)
+                    src = buffer.at[slot].reshape(p.A, p.N2, p.LN).at[:, part]
+                    dst = got.at[me].reshape(p.AP, p.N2, p.LN).at[pl.ds(0, p.A), part]
+                copies[c].append(
+                    remote(src, dst, send.at[c, slot], recv.at[c, slot], {"lon": dest})
+                )
+                if c == 0:
+                    copies[c][-1].start()
+        for group in copies[1:]:
+            for copy in group:
+                copy.start()
         turn(source, got.at[me], me)
         return copies
 
@@ -178,7 +189,7 @@
         pad = jnp.zeros((L, p.PR - p.WP, p.LN), jnp.float32)
         got_a[:, p.WP :, :] = pad
         got_b[:, p.WP :, :] = pad
-    copies_a = exchange(mj, send_a, got_a, a_send, a_recv)
+    copies_a = exchange(mj, send_a, got_a, a_send, a_recv, 1)
 
     to_north.wait()
     to_south.wait()
@@ -231,7 +242,7 @@
             total = here[0] * slope_x + here[1] * slope_y
             adv[f, j, :, :W] = weight * total[:, :W]
 
-    copies_b = exchange(adv, send_b, got_b, b_send, b_recv)
+    copies_b = exchange(adv, send_b, got_b, b_send, b_recv, p.C)
 
     if p.NP > p.N2:
         y_ref[p.N2 * 2 * p.KO :, :] = jnp.zeros(
@@ -239,7 +250,9 @@
         )
     table_copy.wait()
 
-    def first_stage(got):
+    def first_stage(got, c=0, chunks=1):
+        size = p.N2 // chunks // p.U
+
         def step(block, carry):
             for part in range(p.U):
                 n = block * p.U + part
@@ -256,7 +269,7 @@
                 y_ref[pl.ds(pl.multiple_of(n * 2 * p.KO, 8), 2 * p.KO), :] = out
             return carry
 
-        lax.fori_loop(0, p.N2 // p.U, step, 0)
+        lax.fori_loop(c * size, (c + 1) * size, step, 0)
 
     def second_stage(finish):
         table = t2_ref[...]
@@ -291,13 +304,14 @@
         both = f_ref[k] * value
         g_ref[pl.ds(k, p.PO, stride=p.N1), :] = both[: p.PO] + both[p.PO :]
 
-    for copy in copies_a:
+    for copy in copies_a[0]:
         copy.wait()
     first_stage(got_a)
     second_stage(keep)
-    for copy in copies_b:
-        copy.wait()
-    first_stage(got_b)
+    for c, group in enumerate(copies_b):
+        for copy in group:
+            copy.wait()
+        first_stage(got_b, c, p.C)
     second_stage(cross)
 
     for start in range(0, p.NM, 128):
@@ -306,7 +320,10 @@
         wave = lax.broadcasted_iota(jnp.int32, (p.B, 128), 1) + start
         scale = jnp.where(wave == 0, -1.0 / p.NI, -2.0 / p.NI)
         total = (block[: p.B] + block[p.B : 2 * p.B]) * scale
-        out_ref[:, start : start + size] = total[:, :size]
+        turned_out[start // 128] = total
+        for k in range(p.K):
+            rows = turned_out[start // 128, pl.ds(k, p.R, stride=p.K), :]
+            out_ref[k, :, start : start + size] = rows[:, :size]
 
 
 def body(p, *args):
@@ -314,9 +331,9 @@
     f32 = jnp.float32
     vmem = pl.BlockSpec(memory_space=pltpu.VMEM)
     dma = pltpu.SemaphoreType.DMA
-    out = pl.pallas_call(
+    return pl.pallas_call(
         functools.partial(kernel, p),
-        out_shape=jax.ShapeDtypeStruct((p.B, p.NM), f32),
+        out_shape=jax.ShapeDtypeStruct((p.K, p.R, p.NM), f32),
         in_specs=[vmem] * 8 + [pl.BlockSpec(memory_space=pl.ANY), vmem],
         out_specs=vmem,
         scratch_shapes=[
@@ -335,22 +352,22 @@
             pltpu.VMEM((p.NP * 2 * p.KO, p.LN), f32),
             pltpu.VMEM((p.N1, 2 * p.PO, p.LN), f32),
             pltpu.VMEM((max(p.PO * p.N1, up(p.NM, 128)), p.LN), f32),
+            pltpu.VMEM((up(p.NM, 128) // 128, p.B, 128), f32),
             pltpu.VMEM((p.N2, 2 * p.KO, 2 * p.KA), jnp.bfloat16),
             dma(()),
             dma((3,)),
             dma((3,)),
             dma((2,)),
             dma((2,)),
-            dma((p.L - 1,)),
-            dma((p.L - 1,)),
-            dma((p.L - 1,)),
-            dma((p.L - 1,)),
+            dma((1, p.L - 1)),
+            dma((1, p.L - 1)),
+            dma((p.C, p.L - 1)),
+            dma((p.C, p.L - 1)),
         ],
         compiler_params=pltpu.CompilerParams(
             collective_id=0, has_side_effects=True, vmem_limit_bytes=62 * 1024 * 1024
         ),
     )(*args, jnp.asarray(first), jnp.asarray(second))
-    return jnp.transpose(out.reshape(p.R, p.K, p.NM), (1, 0, 2))
 
 
 def solution(mesh):

time: 70.9 us -> 68.2 us (0.962)
  Pallas kernels: 68.7 us -> 66.2 us
    pallas_call x1, Pallas kernels: 68.7 us -> 66.2 us  [body(): pl.pallas_call(functools.partial(kernel, p), out_shape=jax.ShapeDtypeStru...]
    reshape x1 -> x0, local copies, waits for them, and re-layouts: 2.07 us -> none  [body(): return jnp.transpose(out.reshape(p.R, p.K, p.NM), (1, 0, 2))]
    unnamed x0 -> x1, local copies, waits for them, and re-layouts: none -> 1.9 us
where the time goes in v2:
time: 68.2 us; the launch traced here: 68.1 us
  Pallas kernels  66.2 us (97%)
  local copies, waits for them, and re-layouts  1.9 us (3%)
    pallas_call x1, Pallas kernels, body(): pl.pallas_call(functools.partial(kernel, p), out_shape=jax.ShapeDtypeStru...  66.2 us
    unnamed x1, local copies, waits for them, and re-layouts  1.9 us

profile of v2, /device:TPU:1, one launch (start us, length us, event | category | flops | bytes accessed | tf_op | source)
XLA Modules:
  0.0 68.1 jit_solution(4341209457082214665)
XLA Ops:
  0.0 66.2 %shard_map.100 = f32[16,4,2160]{2,1,0:T(4,128)} custom-call(f32[16,16,1080]{2,1,0:T(8,128)} %u_ref.1, f32[16,16,1080]{2,1,0:T(8,128)} %v_ref.1, s32[16,16,1080]{2,1,0:T(8,128)} %um_ref.1, s32[16,16,1080]{2,1,0:T(8,128)} %vm_ref.1, s32[16,16,1080]{2,1,0:T(8,128)} %tm_ref.1, s32[16,1080]{1,0:T(8,128)} %bot_ref.1, f32[16,1080]{1,0:T(8,128)} %idx_ref.1, ...), custom_call_target="tpu_custom_call" | custom-call | tf_op jit(solution)/shard_map/pallas_call | solution.py:334
  66.2 1.9 %copy.12 = f32[16,4,2160]{2,1,0:T(4,128)} copy(f32[16,4,2160]{2,1,0:T(4,128)} %shard_map.100) | data formatting | bytes 1105920

commit v3 on v2

--- a/solution.py
+++ b/solution.py
@@ -42,7 +42,11 @@
         self.KO = up(self.N1, 8)
         self.NP = up(self.N2, 8)
         self.PH = self.N2 // 2
-        self.C = 3 if self.N2 % 24 == 0 and cols % 8 == 0 else 1
+        self.parts = [self.N2]
+        if self.N2 % 8 == 0 and cols % 8 == 0 and self.N2 >= 48:
+            self.parts = [self.N2 - 24, 16, 8]
+        self.C = len(self.parts)
+        self.starts = [sum(self.parts[:c]) for c in range(self.C)]
         self.U = 4 if self.N2 % 4 == 0 else 2
         self.PO = up(self.PH, 8)
         self.NM = self.NI // 2
@@ -72,10 +76,24 @@
         second[0, : self.PH, 1, : self.N2] = np.sin(angle)
         second[1, : self.PH, 0, : self.N2] = -np.sin(angle)
         second[1, : self.PH, 1, : self.N2] = np.cos(angle)
-        second = second.reshape(2 * self.PO, 2 * self.NP)
-        high, low = split_pair(second)
-        second = np.concatenate([high, low, high], axis=1)
-        return first, second
+        pieces = []
+        for start, size in self.spans():
+            piece = second[:, :, :, start : start + size].reshape(2 * self.PO, 2 * size)
+            high, low = split_pair(piece)
+            piece = np.concatenate([high, low, high], axis=1)
+            pieces.append(np.pad(piece, ((0, 0), (0, up(6 * size, 128) - 6 * size))))
+        return first, np.concatenate(pieces, axis=1)
+
+    def spans(self):
+        every = [(0, self.NP)]
+        if self.C > 1:
+            every += list(zip(self.starts, self.parts))
+        return every
+
+    def span(self, index):
+        start, size = self.spans()[index]
+        before = sum(up(6 * width, 128) for _, width in self.spans()[:index])
+        return start, size, before
 
 
 def halves(value):
@@ -85,9 +103,9 @@
 
 
 def kernel(
-    p, u_ref, v_ref, um_ref, vm_ref, tm_ref, bot_ref, idx_ref, idy_ref, t1_hbm, t2_ref, out_ref,
+    p, u_hbm, v_hbm, um_hbm, vm_hbm, tm_hbm, bot_ref, idx_ref, idy_ref, t1_hbm, t2_ref, out_ref,
     mj, adv, inv, south, north, fold, col_out, col_in, send_a, send_b, got_a, got_b, y_ref,
-    f_ref, g_ref, turned_out, t1, table_sem, halo_send, halo_recv, col_send, col_recv, a_send, a_recv,
+    f_ref, p_ref, g_ref, turned_out, u_ref, v_ref, um_ref, vm_ref, tm_ref, t1, in_sem, table_sem, halo_send, halo_recv, col_send, col_recv, a_send, a_recv,
     b_send, b_recv,
 ):
     L, K, J, W, WL = p.L, p.K, p.J, p.W, p.WL
@@ -98,6 +116,14 @@
     partner = L - 1 - me
     at_north = row == p.T - 1
 
+    loads = [
+        pltpu.make_async_copy(src, dst, in_sem.at[at])
+        for at, (src, dst) in enumerate(
+            [(u_hbm, u_ref), (um_hbm, um_ref), (v_hbm, v_ref), (vm_hbm, vm_ref), (tm_hbm, tm_ref)]
+        )
+    ]
+    for load in loads:
+        load.start()
     table_copy = pltpu.make_async_copy(t1_hbm, t1, table_sem)
     table_copy.start()
 
@@ -117,8 +143,13 @@
     inv[0, :, :W] = idx_ref[...] * 0.5
     inv[1, :, :W] = idy_ref[...] * 0.5
     col_out[...] = jnp.zeros_like(col_out)
+    for load in loads[:2]:
+        load.wait()
     for j in range(J):
         mj[0, j, :, :W] = u_ref[:, j, :] * um_ref[:, j, :].astype(jnp.float32)
+    for load in loads[2:4]:
+        load.wait()
+    for j in range(J):
         mj[1, j, :, :W] = v_ref[:, j, :] * vm_ref[:, j, :].astype(jnp.float32)
     for j in range(J):
         for f in range(2):
@@ -163,7 +194,6 @@
 
     def exchange(source, buffer, got, send, recv, chunks):
         copies = [[] for _ in range(chunks)]
-        width = p.N2 // chunks
         for slot, off in enumerate(order):
             dest = lax.rem(me + off, L)
             turn(source, buffer.at[slot], dest)
@@ -171,7 +201,7 @@
                 if chunks == 1:
                     src, dst = buffer.at[slot], got.at[me, pl.ds(0, p.WP)]
                 else:
-                    part = pl.ds(c * width, width)
+                    part = pl.ds(p.starts[c], p.parts[c])
                     src = buffer.at[slot].reshape(p.A, p.N2, p.LN).at[:, part]
                     dst = got.at[me].reshape(p.AP, p.N2, p.LN).at[pl.ds(0, p.A), part]
                 copies[c].append(
@@ -219,6 +249,7 @@
     def _():
         south[...] = jnp.zeros_like(south)
 
+    loads[4].wait()
     lane = lax.broadcasted_iota(jnp.int32, (K, WL), 1)
     level = lax.broadcasted_iota(jnp.int32, (K, W), 0)
     for j in range(J):
@@ -250,8 +281,7 @@
         )
     table_copy.wait()
 
-    def first_stage(got, c=0, chunks=1):
-        size = p.N2 // chunks // p.U
+    def first_stage(got, begin, end):
 
         def step(block, carry):
             for part in range(p.U):
@@ -269,10 +299,11 @@
                 y_ref[pl.ds(pl.multiple_of(n * 2 * p.KO, 8), 2 * p.KO), :] = out
             return carry
 
-        lax.fori_loop(c * size, (c + 1) * size, step, 0)
-
-    def second_stage(finish):
-        table = t2_ref[...]
+        lax.fori_loop(begin // p.U, end // p.U, step, 0)
+
+    def second_stage(finish, index):
+        begin, size, before = p.span(index)
+        table = t2_ref[:, before : before + 6 * size]
 
         def step(block, carry):
             for part in range(2):
@@ -281,7 +312,7 @@
                 for k in ks:
                     y = jnp.concatenate(
                         [
-                            y_ref[pl.ds(k + c * p.KO, p.NP, stride=2 * p.KO), :]
+                            y_ref[pl.ds(2 * p.KO * begin + k + c * p.KO, size, stride=2 * p.KO), :]
                             for c in range(2)
                         ],
                         axis=0,
@@ -300,19 +331,26 @@
     def keep(k, value):
         f_ref[k] = value
 
+    def begin_sum(k, value):
+        p_ref[k] = value
+
+    def add_sum(k, value):
+        p_ref[k] += value
+
     def cross(k, value):
-        both = f_ref[k] * value
+        both = f_ref[k] * (value if p.C == 1 else p_ref[k] + value)
         g_ref[pl.ds(k, p.PO, stride=p.N1), :] = both[: p.PO] + both[p.PO :]
 
     for copy in copies_a[0]:
         copy.wait()
-    first_stage(got_a)
-    second_stage(keep)
+    first_stage(got_a, 0, p.N2)
+    second_stage(keep, 0)
     for c, group in enumerate(copies_b):
         for copy in group:
             copy.wait()
-        first_stage(got_b, c, p.C)
-    second_stage(cross)
+        first_stage(got_b, p.starts[c], p.starts[c] + p.parts[c])
+        finish = cross if c == p.C - 1 else begin_sum if c == 0 else add_sum
+        second_stage(finish, c + 1 if p.C > 1 else 0)
 
     for start in range(0, p.NM, 128):
         size = min(128, p.NM - start)
@@ -330,11 +368,13 @@
     first, second = p.tables()
     f32 = jnp.float32
     vmem = pl.BlockSpec(memory_space=pltpu.VMEM)
+    hbm = pl.BlockSpec(memory_space=pl.ANY)
     dma = pltpu.SemaphoreType.DMA
+    block = (p.K, p.J, p.W)
     return pl.pallas_call(
         functools.partial(kernel, p),
         out_shape=jax.ShapeDtypeStruct((p.K, p.R, p.NM), f32),
-        in_specs=[vmem] * 8 + [pl.BlockSpec(memory_space=pl.ANY), vmem],
+        in_specs=[hbm] * 5 + [vmem] * 3 + [hbm, vmem],
         out_specs=vmem,
         scratch_shapes=[
             pltpu.VMEM((2, p.J, p.K, p.WL), f32),
@@ -351,9 +391,16 @@
             pltpu.VMEM((p.L, p.PR, p.LN), f32),
             pltpu.VMEM((p.NP * 2 * p.KO, p.LN), f32),
             pltpu.VMEM((p.N1, 2 * p.PO, p.LN), f32),
+            pltpu.VMEM((p.N1, 2 * p.PO, p.LN), f32),
             pltpu.VMEM((max(p.PO * p.N1, up(p.NM, 128)), p.LN), f32),
             pltpu.VMEM((up(p.NM, 128) // 128, p.B, 128), f32),
+            pltpu.VMEM(block, f32),
+            pltpu.VMEM(block, f32),
+            pltpu.VMEM(block, jnp.int32),
+            pltpu.VMEM(block, jnp.int32),
+            pltpu.VMEM(block, jnp.int32),
             pltpu.VMEM((p.N2, 2 * p.KO, 2 * p.KA), jnp.bfloat16),
+            dma((5,)),
             dma(()),
             dma((3,)),
             dma((3,)),

time: 68.2 us -> 67.9 us (level); the launches traced: 68.1 us -> 66.8 us
  Pallas kernels: 66.2 us -> 64.9 us
    pallas_call x1, Pallas kernels: 66.2 us -> 64.9 us  [body(): pl.pallas_call(functools.partial(kernel, p), out_shape=jax.ShapeDtypeStru...]
where the time goes in v3:
time: 67.9 us; the launch traced here: 66.8 us
  Pallas kernels  64.9 us (96%)
  local copies, waits for them, and re-layouts  1.9 us (3%)
    pallas_call x1, Pallas kernels, body(): pl.pallas_call(functools.partial(kernel, p), out_shape=jax.ShapeDtypeStru...  64.9 us
    unnamed x1, local copies, waits for them, and re-layouts  1.9 us

profile of v3, /device:TPU:1, one launch (start us, length us, event | category | flops | bytes accessed | tf_op | source)
XLA Modules:
  0.0 66.8 jit_solution(2959891139764963205)
XLA Ops:
  0.0 64.9 %shard_map.100 = f32[16,4,2160]{2,1,0:T(4,128)} custom-call(f32[16,16,1080]{2,1,0:T(8,128)} %u_hbm.1, f32[16,16,1080]{2,1,0:T(8,128)} %v_hbm.1, s32[16,16,1080]{2,1,0:T(8,128)} %um_hbm.1, s32[16,16,1080]{2,1,0:T(8,128)} %vm_hbm.1, s32[16,16,1080]{2,1,0:T(8,128)} %tm_hbm.1, s32[16,1080]{1,0:T(8,128)} %bot_ref.1, f32[16,1080]{1,0:T(8,128)} %idx_ref.1, ...), custom_call_target="tpu_custom_call" | custom-call | tf_op jit(solution)/shard_map/pallas_call | solution.py:374
  64.9 1.9 %copy.12 = f32[16,4,2160]{2,1,0:T(4,128)} copy(f32[16,4,2160]{2,1,0:T(4,128)} %shard_map.100) | data formatting | bytes 1105920

commit v4 on v3

--- a/solution.py
+++ b/solution.py
@@ -143,6 +143,14 @@
     inv[0, :, :W] = idx_ref[...] * 0.5
     inv[1, :, :W] = idy_ref[...] * 0.5
     col_out[...] = jnp.zeros_like(col_out)
+    if p.PR > p.WP:
+        pad = jnp.zeros((L, p.PR - p.WP, p.LN), jnp.float32)
+        got_a[:, p.WP :, :] = pad
+        got_b[:, p.WP :, :] = pad
+    if p.NP > p.N2:
+        y_ref[p.N2 * 2 * p.KO :, :] = jnp.zeros(
+            ((p.NP - p.N2) * 2 * p.KO, p.LN), jnp.float32
+        )
     for load in loads[:2]:
         load.wait()
     for j in range(J):
@@ -151,10 +159,6 @@
         load.wait()
     for j in range(J):
         mj[1, j, :, :W] = v_ref[:, j, :] * vm_ref[:, j, :].astype(jnp.float32)
-    for j in range(J):
-        for f in range(2):
-            col_out[0, f * K : (f + 1) * K, j : j + 1] = mj[f, j, :, W - 1 : W]
-            col_out[1, f * K : (f + 1) * K, j : j + 1] = mj[f, j, :, 0:1]
     pl.semaphore_wait(barrier, L + 1)
 
     def remote(src, dst, send, recv, device):
@@ -168,15 +172,6 @@
     to_fold = remote(mj.at[:, J - 1], fold, halo_send.at[2], halo_recv.at[2], {"lon": partner})
     to_right = remote(col_out.at[0], col_in.at[0], col_send.at[0], col_recv.at[0], {"lon": right})
     to_left = remote(col_out.at[1], col_in.at[1], col_send.at[1], col_recv.at[1], {"lon": left})
-    to_north.start()
-    to_south.start()
-    to_right.start()
-    to_left.start()
-
-    @pl.when(at_north)
-    def _():
-        to_fold.start()
-
     def turn(source, target, dest):
         for start in range(0, W, 128):
             pieces = [
@@ -192,7 +187,7 @@
 
     order = sorted(range(1, L), key=lambda off: abs(off - L // 2))
 
-    def exchange(source, buffer, got, send, recv, chunks):
+    def exchange(source, buffer, got, send, recv, chunks, after_first=None):
         copies = [[] for _ in range(chunks)]
         for slot, off in enumerate(order):
             dest = lax.rem(me + off, L)
@@ -209,17 +204,29 @@
                 )
                 if c == 0:
                     copies[c][-1].start()
+            if slot == 0 and after_first is not None:
+                after_first()
         for group in copies[1:]:
             for copy in group:
                 copy.start()
         turn(source, got.at[me], me)
         return copies
 
-    if p.PR > p.WP:
-        pad = jnp.zeros((L, p.PR - p.WP, p.LN), jnp.float32)
-        got_a[:, p.WP :, :] = pad
-        got_b[:, p.WP :, :] = pad
-    copies_a = exchange(mj, send_a, got_a, a_send, a_recv, 1)
+    def send_edges():
+        for j in range(J):
+            for f in range(2):
+                col_out[0, f * K : (f + 1) * K, j : j + 1] = mj[f, j, :, W - 1 : W]
+                col_out[1, f * K : (f + 1) * K, j : j + 1] = mj[f, j, :, 0:1]
+        to_north.start()
+        to_south.start()
+        to_right.start()
+        to_left.start()
+
+        @pl.when(at_north)
+        def _():
+            to_fold.start()
+
+    copies_a = exchange(mj, send_a, got_a, a_send, a_recv, 1, send_edges)
 
     to_north.wait()
     to_south.wait()
@@ -275,10 +282,6 @@
 
     copies_b = exchange(adv, send_b, got_b, b_send, b_recv, p.C)
 
-    if p.NP > p.N2:
-        y_ref[p.N2 * 2 * p.KO :, :] = jnp.zeros(
-            ((p.NP - p.N2) * 2 * p.KO, p.LN), jnp.float32
-        )
     table_copy.wait()
 
     def first_stage(got, begin, end):

time: 67.9 us -> 68 us (level)
  no operation moved by 1% of the time
where the time goes in v4:
time: 68 us; the launch traced here: 67 us
  Pallas kernels  65.1 us (96%)
  local copies, waits for them, and re-layouts  1.9 us (3%)
    pallas_call x1, Pallas kernels, body(): pl.pallas_call(functools.partial(kernel, p), out_shape=jax.ShapeDtypeStru...  65.1 us
    unnamed x1, local copies, waits for them, and re-layouts  1.9 us

profile of v4, /device:TPU:1, one launch (start us, length us, event | category | flops | bytes accessed | tf_op | source)
XLA Modules:
  0.0 67.0 jit_solution(11793076081798989753)
XLA Ops:
  0.0 65.1 %shard_map.100 = f32[16,4,2160]{2,1,0:T(4,128)} custom-call(f32[16,16,1080]{2,1,0:T(8,128)} %u_hbm.1, f32[16,16,1080]{2,1,0:T(8,128)} %v_hbm.1, s32[16,16,1080]{2,1,0:T(8,128)} %um_hbm.1, s32[16,16,1080]{2,1,0:T(8,128)} %vm_hbm.1, s32[16,16,1080]{2,1,0:T(8,128)} %tm_hbm.1, s32[16,1080]{1,0:T(8,128)} %bot_ref.1, f32[16,1080]{1,0:T(8,128)} %idx_ref.1, ...), custom_call_target="tpu_custom_call" | custom-call | tf_op jit(solution)/shard_map/pallas_call | solution.py:377
  65.1 1.9 %copy.12 = f32[16,4,2160]{2,1,0:T(4,128)} copy(f32[16,4,2160]{2,1,0:T(4,128)} %shard_map.100) | data formatting | bytes 1105920
